TPU v7x, 1024 devices: a whole 4x4x32 slice. The times are simulated.
1024 devices in a mesh: expert: 8 (over x, core), tensor: 128 (over z, y).
Axes of the slice: x: 4, y: 4, z: 32, core: 2. Of those that a mesh axis runs over, the one named last changes fastest.
Arguments:
- tokens: bfloat16 [256, 7168], P('expert', 'tensor'), may hold values from -6 to 6
- routes: int32 [256, 8], P('expert'), may hold values from 0 to 31, all different within a row; in each aligned block of 256 rows (0 to 255, 256 to 511, ...) at most 128 rows name the same one
- gates: bfloat16 [256, 8], P('expert'), may hold values from 0.099609375 to 0.59765625
- w_gate: bfloat16 [32, 2048, 7168], P('expert', 'tensor'), may hold values from -0.0625 to 0.0625
- w_up: bfloat16 [32, 2048, 7168], P('expert', 'tensor'), may hold values from -0.0625 to 0.0625
- w_down: bfloat16 [32, 2048, 7168], P('expert', None, 'tensor'), may hold values from -0.125 to 0.125
Outputs:
- moe_out: bfloat16 [256, 7168], P('expert', 'tensor')
Inputs may be any that keep to these rules, and one draw needn't show every extreme that they name: `routes`: each row names 8 different experts. No expert is named by more than 128 of the 256 rows, and one expert is named by exactly 128 rows.
All inputs are finite; a program needn't handle non-finite values.
Results may differ from a plain program's by a relative error of at most 0.0049.
Values may be sent and summed in bfloat16 or wider, within the bound.
A program may use at most 32 MiB of HBM per device.

v0:
```python
import jax
import jax.numpy as jnp
from jax import lax
from jax.sharding import Mesh
from jax.sharding import PartitionSpec as P

CAP = 128
TENSOR = ("tensor_0", "tensor_1")


def sent_to_all(value, axis):
    length = lax.axis_size(axis)
    return lax.all_to_all(
        jnp.broadcast_to(value[None], (length, *value.shape)), axis, 0, 0, tiled=True
    )


def laid_out(tiles, dim):
    tiles = jnp.moveaxis(tiles, 0, dim)
    lengths = tiles.shape
    return tiles.reshape(*lengths[:dim], lengths[dim] * lengths[dim + 1], *lengths[dim + 2 :])


def collect(value, axis, dim):
    tiles = sent_to_all(value, axis)
    return laid_out(tiles, dim)


def all_blocks(value, axes, order):
    tiles = value
    for k in order:
        tiles = lax.all_gather(tiles, axes[k])
    done = order[::-1]
    back = [done.index(k) for k in range(len(axes))]
    tiles = tiles.transpose(*back, *range(len(axes), tiles.ndim))
    return tiles.reshape(-1, *value.shape)


def gathered_by_axis(value, axes, order, dim):
    return laid_out(all_blocks(value, axes, order), dim)


def in_blocks(value, dim, length):
    lengths = value.shape
    tiles = value.reshape(*lengths[:dim], length, lengths[dim] // length, *lengths[dim + 1 :])
    return jnp.moveaxis(tiles, dim, 0)


def summed_on_arrival(value, axis, dim):
    tiles = in_blocks(value, dim, lax.axis_size(axis))
    arrived = lax.all_to_all(tiles, axis, split_axis=0, concat_axis=0, tiled=True)
    return arrived.sum(axis=0)


def on_device(tokens, routes, gates, w_gate, w_up, w_down):
    exp_dev = w_gate.shape[0]
    experts = exp_dev * lax.axis_size("expert")
    group_index = lax.axis_index("expert")
    expert_ids = jnp.arange(experts, dtype=jnp.int32)
    all_routes = collect(routes, "expert", 0)
    route_hits = all_routes[:, :, None] == expert_ids[None, None, :]
    member = jnp.sum(route_hits.astype(jnp.int32), axis=1)
    before = jnp.cumsum(member, axis=0) - member
    all_slots = jnp.sum(jnp.where(route_hits, before[:, None, :], 0), axis=2)
    col_block = gathered_by_axis(tokens, TENSOR, (0, 1), 1)
    gathered, all_gates = (
        lax.all_gather(col_block, "expert", axis=0, tiled=True),
        lax.all_gather(gates, "expert", axis=0, tiled=True),
    )
    local_ids = all_routes - group_index * exp_dev
    is_local = (local_ids >= 0) & (local_ids < exp_dev)
    slot_id = jnp.where(is_local, local_ids * CAP + all_slots, -1)
    slot_range = jnp.arange(exp_dev * CAP, dtype=jnp.int32)
    matches = slot_id[:, :, None] == slot_range[None, None, :]
    picked = jnp.any(matches, axis=1).astype(jnp.bfloat16)
    mixing = jnp.sum(jnp.where(matches, all_gates.astype(jnp.float32)[:, :, None], 0.0), axis=1)
    slot_rows = lax.dot_general(
        picked, gathered, (((0,), (0,)), ((), ())), preferred_element_type=jnp.float32
    ).astype(jnp.bfloat16)
    slot_rows = slot_rows.reshape(exp_dev, CAP, gathered.shape[1])
    gate_proj = jnp.einsum("ecd,efd->ecf", slot_rows, w_gate, preferred_element_type=jnp.float32)
    up_proj = jnp.einsum("ecd,efd->ecf", slot_rows, w_up, preferred_element_type=jnp.float32)
    hidden = (jax.nn.silu(gate_proj) * up_proj).astype(jnp.bfloat16)
    expert_out = jnp.einsum(
        "ecf,efd->ecd",
        gathered_by_axis(hidden, TENSOR, (0, 1), 2),
        w_down,
        preferred_element_type=jnp.float32,
    )
    expert_out = expert_out.reshape(exp_dev * CAP, w_down.shape[2])
    partial_value = jnp.dot(mixing, expert_out, precision=lax.Precision.HIGHEST)
    result = summed_on_arrival(partial_value, "expert", 0)
    return result.astype(jnp.bfloat16)


def solution(mesh):
    torus = Mesh(
        mesh.devices.reshape(mesh.shape["expert"], 32, 4), ("expert", "tensor_0", "tensor_1")
    )
    placed = (
        P("expert", TENSOR),
        P("expert", None),
        P("expert", None),
        P("expert", TENSOR, None),
        P("expert", TENSOR, None),
        P("expert", None, TENSOR),
    )
    return jax.shard_map(
        on_device, mesh=torus, in_specs=placed, out_specs=P("expert", TENSOR), check_vma=False
    )
```

profile of v0, /device:TPU:1, one launch (start us, length us, event | category | flops | bytes accessed | tf_op | source)
XLA Modules:
  0.0 272.3 jit_solution(5268059561906685158)
XLA Ops:
  6.5 56.5 %all-gather = bf16[1024,56]{1,0:T(8,128)(2,1)S(1)} all-gather(bf16[32,56]{1,0:T(8,128)(2,1)} %param.6), channel_id=2, replica_groups=mesh['expert'=8,'tensor_0'=32,'tensor_1'=4] {'tensor_0'}, dimensions={0}, use_global_device_ids=true | all-gather | bytes 118272 | tf_op jit(solution)/shard_map/all_gather | solution.py:32
  63.0 11.5 %all-gather.1 = bf16[128,32,56]{2,1,0:T(8,128)(2,1)S(1)} all-gather(bf16[32,32,56]{2,1,0:T(8,128)(2,1)S(1)} %bitcast.62), channel_id=3, replica_groups=mesh['expert'=8,'tensor_0'=32,'tensor_1'=4] {'tensor_1'}, dimensions={0}, use_global_device_ids=true | all-gather | bytes 573440 | tf_op jit(solution)/shard_map/all_gather | solution.py:32
  74.5 0.1 copy.59
  74.6 0.4 copy.60
  75.0 2.8 %reshape.54 = bf16[32,7168]{1,0:T(8,128)(2,1)} reshape(bf16[32,128,56]{2,1,0:T(8,128)(2,1)S(1)} %copy.60) | data formatting | bytes 917504 | tf_op jit(solution)/shard_map/reshape | solution.py:21
  77.8 0.7 reshape.69
  78.5 21.9 %all-to-all-start = ((s32[8,1,256]{2,1,0:T(1,128)}), s32[8,1,256]{2,1,0:T(1,128)S(1)}, u32[]{:S(2)}, u32[]{:S(2)}) async-start(s32[8,1,256]{2,1,0:T(1,128)} %reshape.69), calls=%async_computation | async-start | bytes 16384 | tf_op jit(solution)/shard_map/all_to_all | solution.py:13
  100.4 4.6 %all-to-all-done = s32[8,1,256]{2,1,0:T(1,128)S(1)} async-done(((s32[8,1,256]{2,1,0:T(1,128)}), s32[8,1,256]{2,1,0:T(1,128)S(1)}, u32[]{:S(2)}, u32[]{:S(2)}) %all-to-all-start) | async-done | bytes 8224 | tf_op jit(solution)/shard_map/all_to_all | solution.py:13
  105.0 0.5 broadcast.33
  105.5 0.7 reduce.2
  106.4 0.6 reduce-window.6
  107.0 0.2 slice_reduce_fusion
  107.4 0.1 copy.56
  107.5 1.7 fusion
  109.2 24.8 %all-gather.8.cloned.1.call-done = bf16[256,7168]{1,0:T(8,128)(2,1)} async-done(((bf16[32,7168]{1,0:T(8,128)(2,1)}), bf16[256,7168]{1,0:T(8,128)(2,1)}) %all-gather.8.cloned.1.call-update) | async-done | bytes 3670032 | tf_op jit(solution)/shard_map/all_gather | solution.py:67
  134.1 4.1 %convolution_convert_fusion = bf16[512,7168]{1,0:T(8,128)(2,1)S(1)} fusion(pred[256,512]{1,0:T(8,128)(4,1)S(1)} %fusion, bf16[256,7168]{1,0:T(8,128)(2,1)} %all-gather.8.cloned.1.call-done), kind=kOutput, calls=%fused_computation | convolution fusion | flops 1882718208 | bytes 11141120 | tf_op jit(solution)/shard_map/dot_general | solution.py:77
  138.3 2.0 fusion.3
  140.3 2.0 fusion.1
  142.3 51.9 %all-gather.2 = bf16[128,128,16]{1,2,0:T(8,128)(2,1)} all-gather(bf16[4,128,16]{1,2,0:T(8,128)(2,1)S(1)} %fusion.1), channel_id=4, replica_groups=mesh['expert'=8,'tensor_0'=32,'tensor_1'=4] {'tensor_0'}, dimensions={0}, use_global_device_ids=true | all-gather | bytes 540672 | tf_op jit(solution)/shard_map/all_gather | solution.py:32
  194.2 24.8 %all-gather.4 = bf16[8,32,8]{1,2,0:T(8,128)(2,1)S(1)} all-gather(bf16[1,32,8]{1,2,0:T(8,128)(2,1)S(1)} %bitcast.65), channel_id=1, replica_groups=mesh['expert'=8,'tensor_0'=32,'tensor_1'=4] {'expert'}, dimensions={0}, use_global_device_ids=true | all-gather | bytes 4608 | tf_op jit(solution)/shard_map/all_gather | solution.py:68
  219.0 0.1 copy.65
  219.1 1.7 select_reduce_fusion
  220.8 29.4 %all-gather.10.cloned.1.call-done = bf16[128,4,128,16]{2,3,1,0:T(8,128)(2,1)} async-done(((bf16[32,4,128,16]{2,3,1,0:T(8,128)(2,1)}), bf16[128,4,128,16]{2,3,1,0:T(8,128)(2,1)}) %all-gather.10.cloned.1.call-update) | async-done | bytes 2097168 | tf_op jit(solution)/shard_map/all_gather | solution.py:32
  250.2 2.2 copy.61
  252.4 0.5 fusion.4
  253.0 0.6 fusion.5
  253.6 0.2 reshape.71
  253.7 9.7 %all_to_all.10 = f32[8,1,1792]{2,1,0:T(1,128)S(1)} all-to-all(f32[8,1,1792]{2,1,0:T(1,128)S(1)} %reshape.71), channel_id=1, replica_groups=mesh['expert'=8,'tensor_0'=32,'tensor_1'=4] {'expert'}, dimensions={0} | all-to-all | bytes 114688 | tf_op jit(solution)/shard_map/all_to_all | solution.py:51
  263.4 0.5 broadcast.34
  263.9 0.8 reduce.3
  264.7 0.1 reshape.72
  264.9 0.6 reduce_sum.39
  (27 shorter events, 0.5 us)
Async XLA Ops:
  6.5 245.9 %copy-start = (bf16[4,2048,56]{1,2,0:T(8,128)(2,1)S(1)}, bf16[4,2048,56]{1,2,0:T(8,128)(2,1)}, u32[]{:S(2)}) copy-start(bf16[4,2048,56]{1,2,0:T(8,128)(2,1)} %param.11) | copy-start | bytes 2752516
  6.5 71.3 %copy-start.3 = (s32[32,8]{0,1:T(8,128)S(1)}, s32[32,8]{0,1:T(8,128)}, u32[]{:S(2)}) copy-start(s32[32,8]{0,1:T(8,128)} %param.7) | copy-start | bytes 3076
  6.5 127.5 %all-gather.8.cloned.1.call-start = ((), (), s32[]{:S(2)}) async-start(), calls=%async_computation.2 | async-start | bytes 4128768 | tf_op jit(solution)/shard_map/all_gather | solution.py:67
  78.5 26.5 %all-to-all-start = ((s32[8,1,256]{2,1,0:T(1,128)}), s32[8,1,256]{2,1,0:T(1,128)S(1)}, u32[]{:S(2)}, u32[]{:S(2)}) async-start(s32[8,1,256]{2,1,0:T(1,128)} %reshape.69), calls=%async_computation | async-start | bytes 16384 | tf_op jit(solution)/shard_map/all_to_all | solution.py:13
  100.4 149.8 %all-gather.10.cloned.1.call-start = ((), (), s32[]{:S(2)}) async-start(), calls=%async_computation.3 | async-start | bytes 2621440 | tf_op jit(solution)/shard_map/all_gather | solution.py:32
  109.2 29.0 %copy-start.1 = (bf16[4,16,7168]{2,1,0:T(8,128)(2,1)S(1)}, bf16[4,16,7168]{2,1,0:T(8,128)(2,1)}, u32[]{:S(2)}) copy-start(bf16[4,16,7168]{2,1,0:T(8,128)(2,1)} %param.9) | copy-start | bytes 2752516
  138.2 2.0 copy-start.2
  140.3 53.9 %copy-start.4 = (bf16[32,8]{0,1:T(8,128)(2,1)S(1)}, bf16[32,8]{0,1:T(8,128)(2,1)}, u32[]{:S(2)}) copy-start(bf16[32,8]{0,1:T(8,128)(2,1)} %param.8) | copy-start | bytes 1540
Sparse Core Ops, SparseCore 0:
  77.9 56.1 all-gather.7
  194.3 55.8 all-gather.9
where the time goes:
time: 273 us; the launch traced here: 272 us
  blocking collectives  154 us (56%)
  waiting for transfers between devices  58.9 us (22%)
  starting transfers between devices  21.9 us (8%)
  between operations  13.6 us (5%)
  matrix products  9.19 us (3%)
  local copies, waits for them, and re-layouts  8.16 us (3%)
  other arithmetic  6.23 us (2%)
    all_gather x3, blocking collectives, all_blocks(): tiles = lax.all_gather(tiles, axes[k])  120 us
    all_gather x1, waiting for transfers between devices, all_blocks(): tiles = lax.all_gather(tiles, axes[k])  29.4 us
    all_gather x1, waiting for transfers between devices, on_device(): lax.all_gather(col_block, 'expert', axis=0, tiled=True)  24.8 us
    all_gather x1, blocking collectives, on_device(): lax.all_gather(gates, 'expert', axis=0, tiled=True)  24.8 us
    all_to_all x1, starting transfers between devices, sent_to_all(): lax.all_to_all(jnp.broadcast_to(value[None], (length, *value.shape)), axi...  21.9 us
    all_to_all x1, blocking collectives, summed_on_arrival(): lax.all_to_all(tiles, axis, split_axis=0, concat_axis=0, tiled=True)  9.71 us
  transfers between devices with their start and end apart: 3, of which 3 were waited for; matrix products, arithmetic and copies ran while one was open for 2% of the time, Pallas kernels for 0%

commit v1 on v0

v1 whole, which is shorter than its diff:
```python
import functools

import jax
import jax.numpy as jnp
from jax import lax
from jax.experimental import pallas as pl
from jax.experimental.pallas import tpu as pltpu
from jax.sharding import Mesh
from jax.sharding import PartitionSpec as P

CAP = 128
FEAT = 56
ROWS = 16
HID = 16
LOCAL = 4
NEAR = (0, -2, -1, 1)
F32 = jnp.float32
BF16 = jnp.bfloat16
MESH = pl.DeviceIdType.MESH


def iota(shape, dim):
    return lax.broadcasted_iota(jnp.int32, shape, dim)


def ones_where(cond):
    return jnp.where(cond, 1.0, 0.0).astype(BF16)


def dot(a, b):
    return jnp.dot(a, b, preferred_element_type=F32)


def dot_nt(a, b):
    return lax.dot_general(a, b, (((1,), (1,)), ((), ())), preferred_element_type=F32)


def body(sizes, *refs):
    (tok_ref, routes_ref, gates_ref, wg_hbm, wu_hbm, wd_hbm, out_ref,
     xbuf, hbuf, wv, wp, wdv, wdt, pick, acc, yt, pt, mix, comb, rbuf,
     load_sem, xs, xr_, hs, hr, es, er) = refs
    nx, nz, ny = sizes
    top = nz // 8
    x, c = lax.axis_index("x"), lax.axis_index("c")
    z, y = lax.axis_index("z"), lax.axis_index("y")

    def at_x(d):
        return {"x": lax.rem(x + d, nx)}

    def at_y(d):
        return {"y": lax.rem(y + d, ny)}

    def at_z(d):
        return {"z": lax.rem(z + d + nz, nz)}

    def dirs(k):
        return 1 if k in (0, top) else 2

    def start_of(k):
        return 0 if k == 0 else 4 + 8 * (k - 1)

    def part(k, first, count):
        n = dirs(k)
        return pl.ds(start_of(k) + first * n, count * n)

    def one(k, near, way):
        return start_of(k) + near * dirs(k) + way

    def shift_of(k, near, way):
        return NEAR[near] + (4 * k if way or k == top else -4 * k)

    def send(src, dst, send_sem, recv_sem, where):
        pltpu.make_async_remote_copy(
            src_ref=src, dst_ref=dst, send_sem=send_sem, recv_sem=recv_sem,
            device_id=where, device_id_type=MESH,
        ).start()

    def wait(region, sem):
        pltpu.make_async_copy(region, region, sem).wait()

    loads = [
        pltpu.make_async_copy(wg_hbm, wv.at[pl.ds(0, LOCAL)], load_sem.at[0]),
        pltpu.make_async_copy(wu_hbm, wv.at[pl.ds(LOCAL, LOCAL)], load_sem.at[1]),
        pltpu.make_async_copy(wd_hbm, wdv, load_sem.at[2]),
    ]
    for load in loads:
        load.start()

    barrier = pltpu.get_barrier_semaphore()
    peers = [at_z(d) for d in (4, -4, 1, -1, 2, -2)]
    peers += [at_y(d) for d in range(1, ny)]
    peers += [at_x(d) for d in range(1, nx)]
    peers += [{"c": 1 - c}] + [{**at_x(d), "c": 1 - c} for d in range(1, nx)]
    for peer in peers:
        pl.semaphore_signal(barrier, inc=1, device_id=peer, device_id_type=MESH)

    even = (y % 2) == 0
    meta = jnp.where(
        even, routes_ref[...].astype(F32), gates_ref[...].astype(F32)
    ).astype(BF16)
    tile = jnp.zeros((ROWS, 128), F32)
    for half in range(2):
        rows = pl.ds(half * ROWS, ROWS)
        k, lane = iota((FEAT, 128), 0), iota((FEAT, 128), 1)
        tile += dot(tok_ref[rows, :], ones_where(k + 64 * half == lane))
        k, lane = iota((8, 128), 0), iota((8, 128), 1)
        tile += dot(
            meta[half * ROWS:(half + 1) * ROWS], ones_where(k + FEAT + 64 * half == lane)
        )
    xbuf[0, 0, 0, 0] = tile.astype(BF16)

    pl.semaphore_wait(barrier, len(peers))

    def x_far_send(k):
        if k < top:
            send(xbuf.at[0, 0, 0, one(k - 1, 0, 0)], xbuf.at[0, 0, 0, one(k, 0, 0)],
                 xs.at[k, 0], xr_.at[k, 0], at_z(4))
            send(xbuf.at[0, 0, 0, one(k - 1, 0, dirs(k - 1) - 1)],
                 xbuf.at[0, 0, 0, one(k, 0, 1)], xs.at[k, 0], xr_.at[k, 0], at_z(-4))
        else:
            send(xbuf.at[0, 0, 0, one(k - 1, 0, 0)], xbuf.at[0, 0, 0, one(k, 0, 0)],
                 xs.at[k, 0], xr_.at[k, 0], at_z(4))

    def x_far_region(k):
        return xbuf.at[0, 0, 0, part(k, 0, 1)]

    def x_near_send(k):
        for near, d in ((1, 2), (2, 1), (3, -1)):
            send(xbuf.at[0, 0, 0, part(k, 0, 1)], xbuf.at[0, 0, 0, part(k, near, 1)],
                 xs.at[k, 1], xr_.at[k, 1], at_z(d))

    def x_near_region(k):
        return xbuf.at[0, 0, 0, part(k, 1, 3)]

    def x_first_send(k):
        a, b = part(k, 0, 2), part(k, 2, 2)
        for d in range(1, ny):
            send(xbuf.at[0, 0, 0, a], xbuf.at[0, 0, ny - d, a],
                 xs.at[k, 2], xr_.at[k, 2], at_y(d))
        for d in range(1, nx):
            send(xbuf.at[0, 0, 0, b], xbuf.at[0, nx - d, 0, b],
                 xs.at[k, 3], xr_.at[k, 3], at_x(d))

    def x_first_regions(k):
        return (
            xbuf.at[0, 0, pl.ds(1, ny - 1), part(k, 0, 2)],
            xbuf.at[0, pl.ds(1, nx - 1), 0, part(k, 2, 2)],
        )

    def x_second_send(k):
        a, b = part(k, 0, 2), part(k, 2, 2)
        for d in range(1, nx):
            send(xbuf.at[0, 0, :, a], xbuf.at[0, nx - d, :, a],
                 xs.at[k, 4], xr_.at[k, 4], at_x(d))
        for d in range(1, ny):
            send(xbuf.at[0, :, 0, b], xbuf.at[0, :, ny - d, b],
                 xs.at[k, 5], xr_.at[k, 5], at_y(d))

    def x_second_regions(k):
        return (
            xbuf.at[0, pl.ds(1, nx - 1), :, part(k, 0, 2)],
            xbuf.at[0, :, pl.ds(1, ny - 1), part(k, 2, 2)],
        )

    def x_core_send(k):
        g = part(k, 0, 4)
        send(xbuf.at[0, :, :, g], xbuf.at[1, :, :, g],
             xs.at[k, 6], xr_.at[k, 6], {"c": 1 - c})

    def x_core_region(k):
        return xbuf.at[1, :, :, part(k, 0, 4)]

    lanes = 2 * nx * ROWS

    def tile_rows(yr, zi):
        return xbuf[:, :, yr, zi].reshape(lanes, 128)

    def gate_up(k):
        def step(yr, carry):
            total = None
            col = lax.rem(y + yr, ny)
            entries = [(near, way) for near in range(4) for way in range(dirs(k))]
            for p in range(0, len(entries), 2):
                left, right = [], []
                for near, way in entries[p:p + 2]:
                    t = lax.rem(z + shift_of(k, near, way) + nz, nz) * ny + col
                    left.append(wp[t].reshape(256, 128))
                    right.append(tile_rows(yr, one(k, near, way)))
                term = dot_nt(
                    jnp.concatenate(left, axis=1), jnp.concatenate(right, axis=1)
                )
                total = term if total is None else total + term
            acc[...] += total
            return carry

        lax.fori_loop(0, ny, step, 0)

    def prepare_gate_up(i):
        start = FEAT * i
        base, off = start // 128 * 128, start % 128
        width = 128 if off + FEAT <= 128 else 256
        k, lane = iota((width, 256), 0), iota((width, 256), 1)
        j = jnp.where(lane < 128, lane, lane - 192)
        pick[pl.ds(0, width), :] = ones_where((k == j + off) & (j >= 0) & (j < FEAT))

        def step(q, carry):
            cols = pl.ds(pl.multiple_of(q * (16 * FEAT) + base, 128), width)
            got = dot(
                wv[:, :, cols].reshape(2 * LOCAL * HID, width), pick[pl.ds(0, width), :]
            ).astype(BF16)
            wp[q * 16 + i, 0] = got[:, :128]
            wp[q * 16 + i, 1] = got[:, 128:]
            return carry

        lax.fori_loop(0, nz * ny // 16, step, 0)

    def prepare_down(k):
        eye = ones_where(iota((64, FEAT), 0) == iota((64, FEAT), 1))

        def step(e, carry):
            for way in range(dirs(k)):
                rows = []
                for yr in range(ny):
                    for near in range(4):
                        t = lax.rem(z + shift_of(k, near, way) + nz, nz) * ny
                        t = t + lax.rem(y + yr, ny)
                        f = pl.multiple_of(t * HID, HID)
                        rows.append(wdv[e, pl.ds(f, HID), :])
                turned = dot_nt(eye, jnp.concatenate(rows, axis=0))
                wdt[2 * k - (1 if k else 0) + way, e] = turned.astype(BF16)
            return carry

        lax.fori_loop(0, LOCAL, step, 0)

    def prepare_slots():
        r_at = lax.rem(y, 2)
        routes = tile_rows(r_at, 0).astype(F32)
        gates = tile_rows(1 - r_at, 0).astype(F32)
        n = 2 * lanes

        def token_of(i):
            half, i = i // lanes, lax.rem(i, lanes)
            cr, i = i // (nx * ROWS), lax.rem(i, nx * ROWS)
            xr, r = i // ROWS, lax.rem(i, ROWS)
            e = lax.rem(x + xr, nx) * 2 + (c + cr * (1 - 2 * c))
            return e * 32 + half * ROWS + r

        before = ones_where(token_of(iota((n, n), 1)) < token_of(iota((n, n), 0)))
        sel = []
        for half in range(2):
            k = iota((128, 128), 0)
            low = FEAT + 64 * half
            sel.append(ones_where((k >= low) & (k < low + 8)))
        slot_of = iota((n, CAP), 1).astype(F32)
        for e in range(LOCAL):
            name = ((x * 2 + c) * LOCAL + e).astype(F32)
            hit = routes == name
            hit_one = ones_where(hit)
            hit_gate = jnp.where(hit, gates, 0.0).astype(BF16)
            member = jnp.concatenate([dot(hit_one, s) for s in sel], axis=0)
            weight = jnp.concatenate([dot(hit_gate, s) for s in sel], axis=0)
            slot = dot(before, member.astype(BF16))
            picked = (member > 0.5) & (slot == slot_of)
            pt[e] = ones_where(picked)
            mix[:, pl.ds(e * CAP, CAP)] = jnp.where(picked, weight, 0.0).astype(BF16)

    acc[...] = jnp.zeros_like(acc)
    x_far_send(1)
    x_near_send(0)
    loads[0].wait()
    loads[1].wait()
    for tick in range(1, top + 6):
        if tick <= 4:
            for i in range(4 * (tick - 1), 4 * tick):
                prepare_gate_up(i)
        g = tick - 1
        if 0 <= g <= top:
            wait(x_near_region(g), xr_.at[g, 1])
            x_first_send(g)
        g = tick - 2
        if 0 <= g <= top:
            for j, region in enumerate(x_first_regions(g)):
                wait(region, xr_.at[g, 2 + j])
            x_second_send(g)
        g = tick - 3
        if 0 <= g <= top:
            for j, region in enumerate(x_second_regions(g)):
                wait(region, xr_.at[g, 4 + j])
            x_core_send(g)
        if tick <= top:
            wait(x_far_region(tick), xr_.at[tick, 0])
            if tick < top:
                x_far_send(tick + 1)
            x_near_send(tick)
        g = tick - 4
        if 0 <= g <= top:
            wait(x_core_region(g), xr_.at[g, 6])
            if g == 0:
                prepare_slots()
            gate_up(g)
        g = tick - 5
        if g == 0:
            loads[2].wait()

    parts = []
    for half in range(2):
        gate = acc[pl.ds(half * 128, 64), :]
        up = acc[pl.ds(half * 128 + 64, 64), :]
        parts.append((gate / (1.0 + jnp.exp(-gate)) * up).astype(BF16))
    hidden = jnp.concatenate(parts, axis=1)
    for e in range(LOCAL):
        hbuf[0, 0, e] = dot(hidden[e * HID:(e + 1) * HID], pt[e]).astype(BF16)

    ea, eb = pl.ds(0, 3), pl.ds(3, 1)

    def h_far_send(k):
        if k < top:
            send(hbuf.at[0, one(k - 1, 0, 0)], hbuf.at[0, one(k, 0, 0)],
                 hs.at[k, 0], hr.at[k, 0], at_z(4))
            send(hbuf.at[0, one(k - 1, 0, dirs(k - 1) - 1)], hbuf.at[0, one(k, 0, 1)],
                 hs.at[k, 0], hr.at[k, 0], at_z(-4))
        else:
            for way, e, d in ((0, 0, 4), (1, 2, -4)):
                way = min(way, dirs(k - 1) - 1)
                send(hbuf.at[0, one(k - 1, 0, way), pl.ds(e, 2)],
                     hbuf.at[0, one(k, 0, 0), pl.ds(e, 2)],
                     hs.at[k, 0], hr.at[k, 0], at_z(d))

    def h_far_region(k):
        return hbuf.at[0, part(k, 0, 1)]

    def h_first_send(k):
        own = part(k, 0, 1)
        for near, d in ((1, 2), (2, 1), (3, -1)):
            send(hbuf.at[0, own, ea], hbuf.at[0, part(k, near, 1), ea],
                 hs.at[k, 1], hr.at[k, 1], at_z(d))
        for d in range(1, ny):
            send(hbuf.at[0, own, eb], hbuf.at[ny - d, own, eb],
                 hs.at[k, 2], hr.at[k, 2], at_y(d))

    def h_first_regions(k):
        return (
            hbuf.at[0, part(k, 1, 3), ea],
            hbuf.at[pl.ds(1, ny - 1), part(k, 0, 1), eb],
        )

    def h_second_send(k):
        own, group = part(k, 0, 1), part(k, 0, 4)
        for d in range(1, ny):
            send(hbuf.at[0, group, ea], hbuf.at[ny - d, group, ea],
                 hs.at[k, 3], hr.at[k, 3], at_y(d))
        for near, d in ((1, 2), (2, 1), (3, -1)):
            send(hbuf.at[:, own, eb], hbuf.at[:, part(k, near, 1), eb],
                 hs.at[k, 4], hr.at[k, 4], at_z(d))

    def h_second_regions(k):
        return (
            hbuf.at[pl.ds(1, ny - 1), part(k, 0, 4), ea],
            hbuf.at[:, part(k, 1, 3), eb],
        )

    def down(k):
        def step(e, carry):
            total = yt[e]
            for way in range(dirs(k)):
                rows = [
                    hbuf[yr, one(k, near, way), e]
                    for yr in range(ny) for near in range(4)
                ]
                total += dot(
                    wdt[2 * k - (1 if k else 0) + way, e], jnp.concatenate(rows, axis=0)
                )
            yt[e] = total
            return carry

        lax.fori_loop(0, LOCAL, step, 0)

    yt[...] = jnp.zeros_like(yt)
    h_far_send(1)
    h_first_send(0)
    for tick in range(1, top + 3):
        if tick == 1:
            for k in range(top + 1):
                prepare_down(k)
        g = tick - 1
        if 0 <= g <= top:
            for j, region in enumerate(h_first_regions(g)):
                wait(region, hr.at[g, 1 + j])
            h_second_send(g)
        if tick <= top:
            wait(h_far_region(tick), hr.at[tick, 0])
            if tick < top:
                h_far_send(tick + 1)
            h_first_send(tick)
        g = tick - 2
        if 0 <= g <= top:
            for j, region in enumerate(h_second_regions(g)):
                wait(region, hr.at[g, 3 + j])
            down(g)

    y_all = jnp.concatenate([yt[e] for e in range(LOCAL)], axis=1)
    high = y_all.astype(BF16)
    low = (y_all - high.astype(F32)).astype(BF16)
    none = jnp.zeros_like(high)
    total = jnp.zeros((lanes, 128), F32)
    for half in range(2):
        weights = mix[pl.ds(half * lanes, lanes), :]
        for term in (high, low):
            pair = (term, none) if half == 0 else (none, term)
            total += dot_nt(weights, jnp.concatenate(pair, axis=0))
    comb[...] = total.reshape(2 * nx, ROWS, 128)
    for j in range(1, 2 * nx):
        cr, xr = j // nx, j % nx
        where = {"c": 1 - c} if cr else {}
        if xr:
            where = {**where, **at_x(xr)}
        send(comb.at[j], rbuf.at[cr * nx + (nx - xr) % nx], es.at[0], er.at[0], where)
    rest = pl.ds(1, 2 * nx - 1)
    wait(rbuf.at[rest], er.at[0])
    total = comb[0]
    for j in range(1, 2 * nx):
        total += rbuf[j]
    out_ref[pl.ds(0, ROWS), :] = total[:, :FEAT].astype(BF16)
    out_ref[pl.ds(ROWS, ROWS), :] = pltpu.roll(total, 64, 1)[:, :FEAT].astype(BF16)

    for k in range(top + 1):
        if k:
            wait(x_far_region(k), xs.at[k, 0])
            wait(h_far_region(k), hs.at[k, 0])
        wait(x_near_region(k), xs.at[k, 1])
        for j, region in enumerate(x_first_regions(k)):
            wait(region, xs.at[k, 2 + j])
        for j, region in enumerate(x_second_regions(k)):
            wait(region, xs.at[k, 4 + j])
        wait(x_core_region(k), xs.at[k, 6])
        for j, region in enumerate(h_first_regions(k)):
            wait(region, hs.at[k, 1 + j])
        for j, region in enumerate(h_second_regions(k)):
            wait(region, hs.at[k, 3 + j])
    wait(comb.at[rest], es.at[0])


def on_device(sizes, *args):
    nx, nz, ny = sizes
    top = nz // 8
    features = nz * ny * FEAT
    units = nz * ny * HID
    tokens = 2 * nx * 32
    vmem = pl.BlockSpec(memory_space=pltpu.VMEM)
    hbm = pl.BlockSpec(memory_space=pl.ANY)
    dma = pltpu.SemaphoreType.DMA
    return pl.pallas_call(
        functools.partial(body, sizes),
        name="moe_step",
        out_shape=jax.ShapeDtypeStruct((32, FEAT), BF16),
        in_specs=[vmem, vmem, vmem, hbm, hbm, hbm],
        out_specs=vmem,
        scratch_shapes=[
            pltpu.VMEM((2, nx, ny, nz, ROWS, 128), BF16),
            pltpu.VMEM((ny, nz, LOCAL, HID, CAP), BF16),
            pltpu.VMEM((2 * LOCAL, HID, features), BF16),
            pltpu.VMEM((nz * ny, 2, 128, 128), BF16),
            pltpu.VMEM((LOCAL, units, FEAT), BF16),
            pltpu.VMEM((2 * top, LOCAL, 64, 4 * ny * HID), BF16),
            pltpu.VMEM((256, 256), BF16),
            pltpu.VMEM((256, tokens // 2), F32),
            pltpu.VMEM((LOCAL, 64, CAP), F32),
            pltpu.VMEM((LOCAL, tokens, CAP), BF16),
            pltpu.VMEM((tokens, LOCAL * CAP), BF16),
            pltpu.VMEM((2 * nx, ROWS, 128), F32),
            pltpu.VMEM((2 * nx, ROWS, 128), F32),
            dma((3,)),
            dma((top + 1, 7)),
            dma((top + 1, 7)),
            dma((top + 1, 5)),
            dma((top + 1, 5)),
            dma((1,)),
            dma((1,)),
        ],
        compiler_params=pltpu.CompilerParams(
            collective_id=0, has_side_effects=True, vmem_limit_bytes=48 * 1024 * 1024
        ),
    )(*args)


def solution(mesh):
    nz, ny = 32, 4
    nx = mesh.shape["expert"] // 2
    torus = Mesh(mesh.devices.reshape(nx, 2, nz, ny), ("x", "c", "z", "y"))
    experts, tensor = ("x", "c"), ("z", "y")
    placed = (
        P(experts, tensor),
        P(experts, None),
        P(experts, None),
        P(experts, tensor, None),
        P(experts, tensor, None),
        P(experts, None, tensor),
    )
    return jax.shard_map(
        functools.partial(on_device, (nx, nz, ny)),
        mesh=torus, in_specs=placed, out_specs=P(experts, tensor), check_vma=False,
    )
```

time: 273 us -> 105 us (0.38)
  blocking collectives: 154 us -> 0 us
  Pallas kernels: 0 us -> 99.2 us
  waiting for transfers between devices: 58.9 us -> 0 us
  starting transfers between devices: 21.9 us -> 0 us
  between operations: 13.6 us -> 0.04 us
  matrix products: 9.19 us -> 0 us
  other arithmetic: 6.23 us -> 0 us
  local copies, waits for them, and re-layouts: 8.16 us -> 5.39 us
    all_gather x4 -> x0, blocking collectives: 145 us -> none  [the longest x3 120 us: all_blocks(): tiles = lax.all_gather(tiles, axes[k])]
    pallas_call x0 -> x1, Pallas kernels: none -> 99.2 us  [on_device(): pl.pallas_call(functools.partial(body, sizes), name='moe_step', out_shape...]
    all_gather x2 -> x0, waiting for transfers between devices: 54.2 us -> none  [the longest x1 29.4 us: all_blocks(): tiles = lax.all_gather(tiles, axes[k])]
    all_to_all x1 -> x0, starting transfers between devices: 21.9 us -> none  [sent_to_all(): lax.all_to_all(jnp.broadcast_to(value[None], (length, *value.shape)), axi...]
    all_to_all x1 -> x0, blocking collectives: 9.71 us -> none  [summed_on_arrival(): lax.all_to_all(tiles, axis, split_axis=0, concat_axis=0, tiled=True)]
    dot_general x5 -> x0, matrix products: 9.19 us -> none  [the longest x1 4.15 us: on_device(): lax.dot_general(picked, gathered, (((0,), (0,)), ((), ())), preferred_ele...]
    all_to_all x1 -> x0, waiting for transfers between devices: 4.62 us -> none  [sent_to_all(): lax.all_to_all(jnp.broadcast_to(value[None], (length, *value.shape)), axi...]
    unnamed x15 -> x10, local copies, waits for them, and re-layouts: 1.07 us -> 5.39 us
  transfers between devices with their start and end apart: 3 -> 0, of which waited for: 3 -> 0; matrix products, arithmetic and copies ran while one was open for 2% -> 0% of each run, Pallas kernels for 0% -> 0%
where the time goes in v1:
time: 105 us
  Pallas kernels  99.2 us (94%)
  local copies, waits for them, and re-layouts  5.39 us (5%)
    pallas_call x1, Pallas kernels, on_device(): pl.pallas_call(functools.partial(body, sizes), name='moe_step', out_shape...  99.2 us
    unnamed x10, local copies, waits for them, and re-layouts  5.39 us

profile of v1, /device:TPU:1, one launch (start us, length us, event | category | flops | bytes accessed | tf_op | source)
XLA Modules:
  0.0 104.6 jit_solution(14338940999559562440)
XLA Ops:
  0.0 0.0 copy-start
  0.0 0.0 copy-start.2
  0.0 0.8 copy.8.refs_2_
  0.8 0.8 copy.7.refs_1_
  1.6 2.0 %copy.9.refs_5_ = bf16[4,2048,56]{2,1,0:T(8,128)(2,1)S(1)} copy(bf16[4,2048,56]{1,2,0:T(8,128)(2,1)} %param.11) | data formatting | bytes 1835008 | tf_op args[5]
  3.6 0.0 copy-done
  3.6 0.0 copy-done.2
  3.6 0.0 copy-start.1
  3.7 1.2 %copy-done.1 = bf16[4,16,7168]{2,1,0:T(8,128)(2,1)S(1)} copy-done((bf16[4,16,7168]{2,1,0:T(8,128)(2,1)S(1)}, bf16[4,16,7168]{2,1,0:T(8,128)(2,1)}, u32[]{:S(2)}) %copy-start.1) | copy-done | bytes 917528
  4.8 99.2 %moe_step.1 = bf16[32,56]{1,0:T(8,128)(2,1)S(1)} custom-call(bf16[32,56]{1,0:T(8,128)(2,1)S(1)} %copy-done.2, s32[32,8]{1,0:T(8,128)S(1)} %copy.7.refs_1_, bf16[32,8]{1,0:T(8,128)(2,1)S(1)} %copy.8.refs_2_, bf16[4,16,7168]{2,1,0:T(8,128)(2,1)S(1)} %copy-done, bf16[4,16,7168]{2,1,0:T(8,128)(2,1)S(1)} %copy-done.1, bf16[4,2048,56]{2,1,0:T(8,128)(2,1)S(1)} %copy.9.refs_5_), custom_call_target="tpu_custom_call" | custom-call | tf_op jit(solution)/shard_map/moe_step/pallas_call | solution.py:452
  104.0 0.6 copy.11
Async XLA Ops:
  0.0 3.6 %copy-start = (bf16[4,16,7168]{2,1,0:T(8,128)(2,1)S(1)}, bf16[4,16,7168]{2,1,0:T(8,128)(2,1)}, u32[]{:S(2)}) copy-start(bf16[4,16,7168]{2,1,0:T(8,128)(2,1)} %refs_3_.1) | copy-start | bytes 2752516
  0.0 3.6 %copy-start.2 = (bf16[32,56]{1,0:T(8,128)(2,1)S(1)}, bf16[32,56]{1,0:T(8,128)(2,1)}, u32[]{:S(2)}) copy-start(bf16[32,56]{1,0:T(8,128)(2,1)} %refs_0_.1) | copy-start | bytes 10756
  3.6 1.2 %copy-start.1 = (bf16[4,16,7168]{2,1,0:T(8,128)(2,1)S(1)}, bf16[4,16,7168]{2,1,0:T(8,128)(2,1)}, u32[]{:S(2)}) copy-start(bf16[4,16,7168]{2,1,0:T(8,128)(2,1)} %refs_4_.1) | copy-start | bytes 2752516
